TPU v7x, 32 devices: a whole 2x2x4 slice. The times are simulated.
32 devices in a mesh: dp: 4 (over z), expert: 8 (over y, x, core).
Axes of the slice: x: 2, y: 2, z: 4, core: 2. Of those that a mesh axis runs over, the one named last changes fastest.
Arguments:
- frames: bfloat16 [4096, 1024], P(('dp', 'expert')), may hold values from -6 to 6
- norm_gain: float32 [1024], replicated, may hold values from 0.5 to 1.5
- norm_bias: float32 [1024], replicated, may hold values from -3 to 3
- routes: int32 [4096, 2], P(('dp', 'expert')), may hold values from 0 to 15, all different within a row; in each aligned block of 128 rows (0 to 127, 128 to 255, ...) at most 32 rows name the same one
- gate_codes: int32 [4096, 2], P(('dp', 'expert')), may hold values from 1 to 255
- limits: int32 [16], replicated, may hold values from 16 to 32
- up_weight: bfloat16 [32, 1024, 2048], P(('dp', 'expert')), may hold values from -0.1875 to 0.1875
- up_bias: float32 [32, 2048], P(('dp', 'expert')), may hold values from -3 to 3
- down_weight: bfloat16 [32, 2048, 1024], P(('dp', 'expert')), may hold values from -0.09375 to 0.09375
- down_bias: float32 [16, 1024], replicated, may hold values from -2 to 2
Outputs:
- mixed: bfloat16 [4096, 1024], P(('dp', 'expert'))
- load: int32 [16], replicated
Inputs may be any that keep to these rules, and one draw needn't show every extreme that they name: `routes`: in each aligned block of 128 rows (the rows of one device) no expert is named by more than 32 rows, and some block has an expert named by exactly 32 rows; the two entries of a row differ.
All inputs are finite; a program needn't handle non-finite values.
Results may differ from a plain program's by a relative error of at most 0.0051.
Values may be sent and summed in bfloat16 or wider, within the bound.
A program may use at most 64 MiB of HBM per device.

v0:
```python
import functools
import jax
import jax.numpy as jnp
from jax import lax
from jax.experimental import pallas as pl
from jax.experimental.pallas import tpu as pltpu
from jax.sharding import PartitionSpec as P

epsilon = 1e-05
TILE = 1024
PIECES = 2


def paired(value, step, size):
    bit = 1
    out = value
    while bit < size:
        if step & bit:
            out = out + bit - 2 * bit * lax.rem(value // bit, 2)
        bit *= 2
    return out


def moe_kernel(
    owners,
    holders,
    groups,
    capacity,
    limits,
    frames,
    gain,
    bias,
    routes,
    codes,
    up_weight,
    up_bias,
    down_weight,
    down_bias,
    mixed,
    load,
    up_all,
    down_all,
    bias_all,
    facts,
    shared,
    outgoing,
    incoming,
    answers,
    returned,
    halves,
    counts,
    class_count,
    group_counts,
    mix_high,
    mix_low,
    total,
    own_sem,
    weight_send,
    weight_recv,
    fact_send,
    fact_recv,
    shared_send,
    shared_recv,
    slot_send,
    slot_recv,
    back_send,
    back_recv,
    half_send,
    half_recv,
    count_send,
    count_recv,
    group_send,
    group_recv,
):
    row = lax.axis_index("dp")
    column = lax.axis_index("expert")
    near = holders // groups
    flat = row * holders + column
    place = flat // groups
    member = lax.rem(flat, groups)
    band = place // near
    spot = lax.rem(place, near)
    frame_count, width = frames.shape
    slots = near * capacity
    hidden_units = up_weight.shape[2]
    bands = owners // 2
    pieces = shared.shape[1]
    part = width // pieces
    steps = owners * near
    kept_steps = bands * near

    def address(expert, group):
        number = expert * groups + group
        return (number // holders, lax.rem(number, holders))

    def remote(source, target, send, recv, to):
        return pltpu.make_async_remote_copy(
            src_ref=source,
            dst_ref=target,
            send_sem=send,
            recv_sem=recv,
            device_id=to,
            device_id_type=pl.DeviceIdType.MESH,
        )

    spots = [paired(spot, j, near) for j in range(near)]
    to_band = [paired(band, k, owners) for k in range(owners)]
    ahead = [to_band[k] * near + spots[j] for k in range(owners) for j in range(near)]
    peers = [lax.rem(member + t, groups) for t in range(groups)]

    barrier = pltpu.get_barrier_semaphore()
    for r in range(1, steps):
        pl.semaphore_signal(
            barrier, inc=1, device_id=address(ahead[r], member), device_id_type=pl.DeviceIdType.MESH
        )
    for t in range(1, groups):
        pl.semaphore_signal(
            barrier, inc=1, device_id=address(place, peers[t]), device_id_type=pl.DeviceIdType.MESH
        )
    own = [
        pltpu.make_async_copy(up_weight.at[0], up_all.at[0], own_sem.at[0]),
        pltpu.make_async_copy(down_weight.at[0], down_all.at[0], own_sem.at[1]),
    ]
    for copy in own:
        copy.start()
    bias_all[0] = up_bias[...]
    facts[0, 0:2, :] = routes[...]
    facts[0, 2:4, :] = codes[...]
    facts[0, 4:8, :] = jnp.zeros((4, frame_count), jnp.int32)

    values = frames[...].astype(jnp.float32)
    center = jnp.mean(values, axis=-1, keepdims=True)
    shifted = values - center
    spread = jnp.mean(shifted * shifted, axis=-1, keepdims=True)
    normed = (shifted * lax.rsqrt(spread + epsilon) * gain[...] + bias[...]).astype(jnp.bfloat16)
    for c in range(pieces):
        shared[0, c] = normed[:, c * part : (c + 1) * part]

    square = (frame_count, frame_count)
    across = lax.broadcasted_iota(jnp.int32, square, 1)
    along = lax.broadcasted_iota(jnp.int32, square, 0)
    earlier = jnp.where(across < along, 1.0, 0.0).astype(jnp.bfloat16)
    diagonal = across == along
    lanes = lax.broadcasted_iota(jnp.int32, (frame_count, slots), 1)
    slot_of = lax.rem(lanes, capacity).astype(jnp.float32)
    line = lax.broadcasted_iota(jnp.int32, (1, slots), 1) // capacity

    def places(u):
        def upright(i):
            lying = facts[u, i : i + 1, :].astype(jnp.float32)
            return jnp.sum(jnp.where(diagonal, lying, 0.0), axis=1, keepdims=True)

        first, second = upright(0).astype(jnp.int32), upright(1).astype(jnp.int32)
        first_code, second_code = upright(2), upright(3)
        code_sum = first_code + second_code
        first_share, second_share = first_code / code_sum, second_code / code_sum
        picks = []
        tally = jnp.zeros((frame_count, 128), jnp.float32)
        for k in range(bands):
            expert_of = lanes // capacity + to_band[k] * near
            hit_first, hit_second = first == expert_of, second == expert_of
            hits = jnp.where(hit_first | hit_second, 1.0, 0.0)
            rank = jnp.dot(earlier, hits.astype(jnp.bfloat16), preferred_element_type=jnp.float32)
            bound = jnp.zeros((1, slots), jnp.int32)
            for s in range(near):
                bound = jnp.where(line == s, limits[to_band[k] * near + s], bound)
            fits = (rank == slot_of) & (rank < bound.astype(jnp.float32))
            chosen = jnp.where(fits, hits, 0.0)
            picks.append(chosen.astype(jnp.bfloat16))
            mix = chosen * jnp.where(hit_first, first_share, second_share)
            high = mix.astype(jnp.bfloat16)
            mix_high[u, k] = high
            mix_low[u, k] = (mix - high.astype(jnp.float32)).astype(jnp.bfloat16)
            to_lane = (
                lax.broadcasted_iota(jnp.int32, (slots, 128), 0) // capacity + to_band[k] * near
                == lax.broadcasted_iota(jnp.int32, (slots, 128), 1)
            )
            tally = tally + jnp.dot(
                picks[k],
                jnp.where(to_lane, 1.0, 0.0).astype(jnp.bfloat16),
                preferred_element_type=jnp.float32,
            )
        return picks, jnp.sum(tally, axis=0, keepdims=True)

    def fill(u, k, c, picked, source):
        rows = lax.dot_general(
            picked, source, (((0,), (0,)), ((), ())), preferred_element_type=jnp.float32
        )
        outgoing[u, k * near : (k + 1) * near, :, c * part : (c + 1) * part] = rows.astype(
            jnp.bfloat16
        ).reshape(near, capacity, part)

    def slot_copy(u, r, c):
        k, j = r // near, r % near
        columns = pl.ds(c * part, part)
        return remote(
            outgoing.at[u, k * near + spots[j], :, columns],
            incoming.at[u, r, :, columns],
            slot_send.at[u, r, c],
            slot_recv.at[u, r, c],
            address(ahead[r], member),
        )

    send_order = [r for k in range(bands - 1, -1, -1) for r in range(k * near, (k + 1) * near) if r]

    pl.semaphore_wait(barrier, steps - 1 + groups - 1)
    other = address(to_band[bands] * near + spot, member)
    fact_copy = remote(facts.at[0], facts.at[1], fact_send, fact_recv, other)
    fact_copy.start()
    shared_copies = [
        remote(shared.at[0, c], shared.at[1, c], shared_send.at[c], shared_recv.at[c], other)
        for c in range(pieces)
    ]
    for copy in shared_copies:
        copy.start()
    weight_copies = []
    for t in range(1, groups):
        to = address(place, peers[t])
        weight_copies += [
            remote(bias_all.at[0], bias_all.at[t], weight_send.at[t, 0], weight_recv.at[t, 0], to),
            remote(up_weight.at[0], up_all.at[t], weight_send.at[t, 1], weight_recv.at[t, 1], to),
            remote(down_weight.at[0], down_all.at[t], weight_send.at[t, 2], weight_recv.at[t, 2], to),
        ]
    for copy in weight_copies:
        copy.start()

    own_picks, own_tally = places(0)
    for k in range(bands - 1, -1, -1):
        for c in range(pieces):
            fill(0, k, c, own_picks[k], normed[:, c * part : (c + 1) * part])
    for r in send_order:
        for c in range(pieces):
            slot_copy(0, r, c).start()
    incoming[0, 0] = outgoing[0, spot]

    fact_copy.wait()
    other_picks, other_tally = places(1)
    for c in range(pieces):
        shared_copies[c].wait()
        for k in range(bands - 1, -1, -1):
            fill(1, k, c, other_picks[k], shared[1, c])
        for r in send_order:
            slot_copy(1, r, c).start()
    incoming[1, 0] = outgoing[1, spot]

    counts[0] = jnp.broadcast_to((own_tally + other_tally).astype(jnp.int32), (8, 128))
    count_copies = [
        remote(counts.at[0], counts.at[r], count_send.at[r], count_recv.at[r], address(ahead[r], member))
        for r in range(1, steps)
    ]

    for copy in count_copies:
        copy.start()

    out_bias = down_bias[pl.ds(place, 1), :]
    tile = min(TILE, hidden_units)
    tiles = hidden_units // tile
    for copy in own:
        copy.wait()
    for copy in weight_copies:
        copy.wait()

    def back_copy(u, r):
        k = r // near
        return remote(
            answers.at[u, r],
            returned.at[u, k * near + spot],
            back_send.at[u, r],
            back_recv.at[u, r],
            address(ahead[r], member),
        )

    def answer(u, k):
        for r in range(k * near, (k + 1) * near):
            if r:
                for c in range(pieces):
                    slot_copy(u, r, c).wait_recv()
        rows = incoming[u, k * near : (k + 1) * near].reshape(slots, width)
        total[0:slots] = jnp.broadcast_to(out_bias, (slots, width))

        def step(i, carry):
            t = i // tiles
            begin = pl.multiple_of(lax.rem(i, tiles) * tile, tile)
            pre = jnp.dot(
                rows, up_all[t, :, pl.ds(begin, tile)], preferred_element_type=jnp.float32
            )
            pre = pre + bias_all[t, :, pl.ds(begin, tile)]
            hidden = (0.5 * pre * (1.0 + lax.erf(pre * 0.7071067811865476))).astype(jnp.bfloat16)
            total[0:slots] += jnp.dot(
                hidden, down_all[t, pl.ds(begin, tile), :], preferred_element_type=jnp.float32
            )
            return carry

        lax.fori_loop(0, groups * tiles, step, 0)
        answers[u, k * near : (k + 1) * near] = (
            total[0:slots].astype(jnp.bfloat16).reshape(near, capacity, width)
        )
        for r in range(k * near, (k + 1) * near):
            if r:
                back_copy(u, r).start()

    def arrived(u):
        for r in range(1, kept_steps):
            k, j = r // near, r % near
            remote(
                answers.at[u, r],
                returned.at[u, k * near + spots[j]],
                back_send.at[u, r],
                back_recv.at[u, r],
                address(ahead[r], member),
            ).wait_recv()
        returned[u, spot] = answers[u, 0]

    def mixture(u, c):
        result = jnp.zeros((frame_count, part), jnp.float32)
        for k in range(bands):
            picked = returned[u, k * near : (k + 1) * near, :, c * part : (c + 1) * part]
            picked = picked.reshape(slots, part)
            result = (
                result
                + jnp.dot(mix_high[u, k], picked, preferred_element_type=jnp.float32)
                + jnp.dot(mix_low[u, k], picked, preferred_element_type=jnp.float32)
            )
        return result

    answer(0, 0)
    for k in range(bands - 1, -1, -1):
        answer(1, k)
    for k in range(bands - 1, 0, -1):
        answer(0, k)

    arrived(1)
    half_copies = [
        remote(halves.at[0, c], halves.at[1, c], half_send.at[c], half_recv.at[c], other)
        for c in range(pieces)
    ]
    for c in range(pieces):
        halves[0, c] = mixture(1, c).astype(jnp.bfloat16)
        half_copies[c].start()

    for copy in count_copies:
        copy.wait()
    class_total = counts[0]
    for r in range(1, steps):
        class_total = class_total + counts[r]
    class_count[...] = class_total
    group_copies = [
        remote(class_count, group_counts.at[t], group_send.at[t], group_recv.at[t], address(place, peers[t]))
        for t in range(1, groups)
    ]
    for copy in group_copies:
        copy.start()

    arrived(0)
    for c in range(pieces):
        total[0:frame_count, c * part : (c + 1) * part] = frames[
            :, c * part : (c + 1) * part
        ].astype(jnp.float32) + mixture(0, c)
    for copy in group_copies:
        copy.wait()
    everything = class_count[...]
    for t in range(1, groups):
        everything = everything + group_counts[t]
    load[...] = everything
    for u in range(2):
        for r in range(1, kept_steps):
            for c in range(pieces):
                slot_copy(u, r, c).wait_send()
            back_copy(u, r).wait_send()
    for c in range(pieces):
        half_copies[c].wait()
        mixed[:, c * part : (c + 1) * part] = (
            total[0:frame_count, c * part : (c + 1) * part] + halves[1, c].astype(jnp.float32)
        ).astype(jnp.bfloat16)


def per_device(
    frames,
    norm_gain,
    norm_bias,
    routes,
    gate_codes,
    limits,
    up_weight,
    up_bias,
    down_weight,
    down_bias,
):
    owners = lax.axis_size("dp")
    holders = lax.axis_size("expert")
    expert_total = down_bias.shape[0]
    groups = owners * holders // expert_total
    frame_count, width = frames.shape
    capacity = 4 * frame_count // expert_total
    hidden_units = up_weight.shape[2]
    near = holders // groups
    slots = near * capacity
    vmem = pl.BlockSpec(memory_space=pltpu.VMEM)
    anywhere = pl.BlockSpec(memory_space=pl.ANY)
    kept_steps = expert_total // 2
    blocks = (2, kept_steps, capacity, width)
    halved = (2, PIECES, frame_count, width // PIECES)
    dma = pltpu.SemaphoreType.DMA
    mixed, load = pl.pallas_call(
        functools.partial(moe_kernel, owners, holders, groups, capacity),
        out_shape=(
            jax.ShapeDtypeStruct((frame_count, width), jnp.bfloat16),
            jax.ShapeDtypeStruct((8, 128), jnp.int32),
        ),
        in_specs=[
            pl.BlockSpec(memory_space=pltpu.SMEM),
            vmem,
            vmem,
            vmem,
            vmem,
            vmem,
            anywhere,
            vmem,
            anywhere,
            vmem,
        ],
        out_specs=(vmem, vmem),
        scratch_shapes=[
            pltpu.VMEM((groups, width, hidden_units), jnp.bfloat16),
            pltpu.VMEM((groups, hidden_units, width), jnp.bfloat16),
            pltpu.VMEM((groups, 1, hidden_units), jnp.float32),
            pltpu.VMEM((2, 8, frame_count), jnp.int32),
            pltpu.VMEM(halved, jnp.bfloat16),
            pltpu.VMEM(blocks, jnp.bfloat16),
            pltpu.VMEM(blocks, jnp.bfloat16),
            pltpu.VMEM(blocks, jnp.bfloat16),
            pltpu.VMEM(blocks, jnp.bfloat16),
            pltpu.VMEM(halved, jnp.bfloat16),
            pltpu.VMEM((expert_total, 8, 128), jnp.int32),
            pltpu.VMEM((8, 128), jnp.int32),
            pltpu.VMEM((groups, 8, 128), jnp.int32),
            pltpu.VMEM((2, owners // 2, frame_count, slots), jnp.bfloat16),
            pltpu.VMEM((2, owners // 2, frame_count, slots), jnp.bfloat16),
            pltpu.VMEM((max(slots, frame_count), width), jnp.float32),
            dma((2,)),
            dma((groups, 3)),
            dma((groups, 3)),
            dma(()),
            dma(()),
            dma((PIECES,)),
            dma((PIECES,)),
            dma((2, kept_steps, PIECES)),
            dma((2, kept_steps, PIECES)),
            dma((2, kept_steps)),
            dma((2, kept_steps)),
            dma((PIECES,)),
            dma((PIECES,)),
            dma((expert_total,)),
            dma((expert_total,)),
            dma((groups,)),
            dma((groups,)),
        ],
        compiler_params=pltpu.CompilerParams(
            collective_id=0, has_side_effects=True, vmem_limit_bytes=56 * 1024 * 1024
        ),
        name="moe",
    )(
        limits,
        frames,
        norm_gain.reshape(1, width),
        norm_bias.reshape(1, width),
        routes.T,
        gate_codes.T,
        up_weight,
        up_bias,
        down_weight,
        down_bias,
    )
    return (mixed, load[0, :expert_total])


def solution(mesh):
    in_specs = (
        P(("dp", "expert"), None),
        P(),
        P(),
        P(("dp", "expert"), None),
        P(("dp", "expert"), None),
        P(),
        P(("dp", "expert"), None, None),
        P(("dp", "expert"), None),
        P(("dp", "expert"), None, None),
        P(),
    )
    out_specs = (P(("dp", "expert"), None), P())
    return jax.shard_map(
        per_device, mesh=mesh, in_specs=in_specs, out_specs=out_specs, check_vma=False
    )
```

profile of v0, /device:TPU:0, one launch (start us, length us, event | category | flops | bytes accessed | tf_op | source)
XLA Modules:
  0.0 58.1 jit_solution(15050918135767624439)
XLA Ops:
  0.6 54.5 %moe.1 = (bf16[128,1024]{1,0:T(8,128)(2,1)}, s32[8,128]{1,0:T(8,128)}) custom-call(s32[16]{0:T(128)} %limits.1, bf16[128,1024]{1,0:T(8,128)(2,1)} %frames.1, f32[1,1024]{1,0:T(1,128)} %bitcast.6, f32[1,1024]{1,0:T(1,128)} %bitcast.7, s32[2,128]{1,0:T(2,128)} %bitcast.8, s32[2,128]{1,0:T(2,128)} %bitcast.9, bf16[1,1024,2048]{2,1,0:T(8,128)(2,1)} %up_weight.1, ...), custom_call_target="tpu_custom_call" | custom-call | tf_op jit(solution)/shard_map/moe/pallas_call | solution.py:404
  55.2 1.2 %slice_bitcast_fusion = s32[16]{0:T(128)} fusion(s32[8,128]{1,0:T(8,128)} %get-tuple-element.5), kind=kLoop, calls=%fused_computation | loop fusion | bytes 128 | tf_op jit(solution)/shard_map/squeeze | solution.py:474
  56.4 1.7 %copy.13 = bf16[128,1024]{1,0:T(8,128)(2,1)} copy(bf16[128,1024]{1,0:T(8,128)(2,1)} %get-tuple-element.8) | data formatting | bytes 524288
where the time goes:
time: 58.3 us; the launch traced here: 58.1 us
  Pallas kernels  54.5 us (93%)
  local copies, waits for them, and re-layouts  2.86 us (5%)
  between operations  0.64 us (1%)
    pallas_call x1, Pallas kernels, per_device(): pl.pallas_call(functools.partial(moe_kernel, owners, holders, groups, cap...  54.5 us
    unnamed x1, local copies, waits for them, and re-layouts  1.67 us
    squeeze x1, local copies, waits for them, and re-layouts, per_device(): return (mixed, load[0, :expert_total])  1.2 us

commit v1 on v0

v1 whole, which is shorter than its diff:
```python
import functools
import jax
import jax.numpy as jnp
from jax import lax
from jax.experimental import pallas as pl
from jax.experimental.pallas import tpu as pltpu
from jax.sharding import PartitionSpec as P

epsilon = 1e-05
TILE = 512
PIECES = 4
CHUNKS = 2


def paired(value, step, size):
    bit = 1
    out = value
    while bit < size:
        if step & bit:
            out = out + bit - 2 * bit * lax.rem(value // bit, 2)
        bit *= 2
    return out


def moe_kernel(
    owners,
    holders,
    groups,
    capacity,
    limits,
    frames,
    gain,
    bias,
    routes,
    codes,
    up_weight,
    up_bias,
    down_weight,
    down_bias,
    mixed,
    load,
    up_all,
    down_all,
    bias_all,
    facts,
    shared,
    outgoing,
    incoming,
    hidden,
    answers,
    returned,
    halves,
    counts,
    class_count,
    group_counts,
    mix_high,
    mix_low,
    total,
    own_sem,
    weight_send,
    weight_recv,
    fact_send,
    fact_recv,
    shared_send,
    shared_recv,
    slot_send,
    slot_recv,
    back_send,
    back_recv,
    half_send,
    half_recv,
    count_send,
    count_recv,
    group_send,
    group_recv,
):
    row = lax.axis_index("dp")
    column = lax.axis_index("expert")
    near = holders // groups
    flat = row * holders + column
    place = flat // groups
    member = lax.rem(flat, groups)
    band = place // near
    spot = lax.rem(place, near)
    early = lax.rem(member, 2) == 0
    late = lax.rem(member, 2) == 1
    frame_count, width = frames.shape
    hidden_units = up_weight.shape[2]
    bands = owners // 2
    steps = owners * near
    kept_steps = bands * near
    slots = kept_steps * capacity
    block = near * capacity
    part = width // PIECES
    chunk = width // CHUNKS
    scope = jax.named_scope

    def address(expert, group):
        number = expert * groups + group
        return (number // holders, lax.rem(number, holders))

    def remote(source, target, send, recv, to):
        return pltpu.make_async_remote_copy(
            src_ref=source,
            dst_ref=target,
            send_sem=send,
            recv_sem=recv,
            device_id=to,
            device_id_type=pl.DeviceIdType.MESH,
        )

    spots = [paired(spot, j, near) for j in range(near)]
    to_band = [paired(band, k, owners) for k in range(owners)]
    ahead = [to_band[k] * near + spots[j] for k in range(owners) for j in range(near)]
    peers = [lax.rem(member + t, groups) for t in range(groups)]

    barrier = pltpu.get_barrier_semaphore()
    for r in range(1, steps):
        pl.semaphore_signal(
            barrier, inc=1, device_id=address(ahead[r], member), device_id_type=pl.DeviceIdType.MESH
        )
    for t in range(1, groups):
        pl.semaphore_signal(
            barrier, inc=1, device_id=address(place, peers[t]), device_id_type=pl.DeviceIdType.MESH
        )
    own = [
        pltpu.make_async_copy(up_weight.at[0], up_all.at[0], own_sem.at[0]),
        pltpu.make_async_copy(down_weight.at[0], down_all.at[0], own_sem.at[1]),
    ]
    for copy in own:
        copy.start()
    bias_all[0] = up_bias[...]
    facts[0, 0:2, :] = routes[...]
    facts[0, 2:4, :] = codes[...]
    facts[0, 4:8, :] = jnp.zeros((4, frame_count), jnp.int32)

    values = frames[...].astype(jnp.float32)
    center = jnp.mean(values, axis=-1, keepdims=True)
    shifted = values - center
    spread = jnp.mean(shifted * shifted, axis=-1, keepdims=True)
    normed = (shifted * lax.rsqrt(spread + epsilon) * gain[...] + bias[...]).astype(jnp.bfloat16)
    for c in range(PIECES):
        shared[0, c] = normed[:, c * part : (c + 1) * part]

    square = (frame_count, frame_count)
    across = lax.broadcasted_iota(jnp.int32, square, 1)
    along = lax.broadcasted_iota(jnp.int32, square, 0)
    earlier = jnp.where(across < along, 1.0, 0.0).astype(jnp.bfloat16)
    diagonal = across == along
    lane = lax.broadcasted_iota(jnp.int32, (1, slots), 1)
    line = lane // capacity
    slot_of = lax.rem(lane, capacity).astype(jnp.float32)

    def expert_at(q):
        return to_band[q // near] * near + q % near

    def experts(numbers):
        out = jnp.zeros(numbers.shape, jnp.int32)
        for q in range(kept_steps):
            out = jnp.where(numbers == q, expert_at(q), out)
        return out

    expert_of = experts(line)
    bound = jnp.zeros((1, slots), jnp.int32)
    for q in range(kept_steps):
        bound = jnp.where(line == q, limits[expert_at(q)], bound)
    bound = bound.astype(jnp.float32)
    tall = lax.broadcasted_iota(jnp.int32, (slots, 128), 0) // capacity
    to_lane = experts(tall) == lax.broadcasted_iota(jnp.int32, (slots, 128), 1)
    to_lane = jnp.where(to_lane, 1.0, 0.0).astype(jnp.bfloat16)

    def places(u):
        def upright(i):
            lying = facts[u, i : i + 1, :].astype(jnp.float32)
            return jnp.sum(jnp.where(diagonal, lying, 0.0), axis=1, keepdims=True)

        first, second = upright(0).astype(jnp.int32), upright(1).astype(jnp.int32)
        first_code, second_code = upright(2), upright(3)
        code_sum = first_code + second_code
        first_share, second_share = first_code / code_sum, second_code / code_sum
        hit_first, hit_second = first == expert_of, second == expert_of
        hits = jnp.where(hit_first | hit_second, 1.0, 0.0)
        rank = jnp.dot(earlier, hits.astype(jnp.bfloat16), preferred_element_type=jnp.float32)
        fits = (rank == slot_of) & (rank < bound)
        chosen = jnp.where(fits, hits, 0.0)
        picked = chosen.astype(jnp.bfloat16)
        mix = chosen * jnp.where(hit_first, first_share, second_share)
        high = mix.astype(jnp.bfloat16)
        mix_high[u] = high
        mix_low[u] = (mix - high.astype(jnp.float32)).astype(jnp.bfloat16)
        tally = jnp.dot(picked, to_lane, preferred_element_type=jnp.float32)
        return picked, jnp.sum(tally, axis=0, keepdims=True)

    def fill(u, begin, size, picked, source):
        rows = lax.dot_general(
            picked, source, (((0,), (0,)), ((), ())), preferred_element_type=jnp.float32
        )
        outgoing[u, :, :, begin : begin + size] = rows.astype(jnp.bfloat16).reshape(
            kept_steps, capacity, size
        )

    def slot_copy(u, r, c):
        k, j = r // near, r % near
        columns = pl.ds(c * part, part) if u else pl.ds(0, width)
        return remote(
            outgoing.at[u, k * near + spots[j], :, columns],
            incoming.at[u, r, :, columns],
            slot_send.at[u, r, c],
            slot_recv.at[u, r, c],
            address(ahead[r], member),
        )

    inside = list(range(1, near))
    outside = list(range(near, kept_steps))

    with scope("barrier"):
        pl.semaphore_wait(barrier, steps - 1 + groups - 1)
    other = address(to_band[bands] * near + spot, member)
    fact_copy = remote(facts.at[0], facts.at[1], fact_send, fact_recv, other)
    fact_copy.start()
    shared_copies = [
        remote(shared.at[0, c], shared.at[1, c], shared_send.at[c], shared_recv.at[c], other)
        for c in range(PIECES)
    ]

    @pl.when(early)
    def _():
        for copy in shared_copies:
            copy.start()

    weight_copies = []
    for t in range(1, groups):
        to = address(place, peers[t])
        weight_copies.append([
            remote(bias_all.at[0], bias_all.at[t], weight_send.at[t, 0], weight_recv.at[t, 0], to),
            remote(up_weight.at[0], up_all.at[t], weight_send.at[t, 1], weight_recv.at[t, 1], to),
            remote(down_weight.at[0], down_all.at[t], weight_send.at[t, 2], weight_recv.at[t, 2], to),
        ])
    for i in range(3):
        for copies in weight_copies:
            copies[i].start()

    with scope("fill0"):
        own_picks, own_tally = places(0)
        fill(0, 0, width, own_picks, normed)
    for r in inside:
        slot_copy(0, r, 0).start()
    incoming[0, 0] = outgoing[0, spot]

    @pl.when(late)
    def _():
        for r in outside:
            slot_copy(0, r, 0).start()
        with scope("slotsend"):
            for r in outside:
                slot_copy(0, r, 0).wait_send()
        for copy in shared_copies:
            copy.start()

    with scope("factwait"):
        fact_copy.wait()
    with scope("places1"):
        other_picks, other_tally = places(1)
    for c in range(PIECES):
        with scope(f"sharedwait{c}"):
            shared_copies[c].wait_recv()
        fill(1, c * part, part, other_picks, shared[1, c])
        for r in outside + inside:
            slot_copy(1, r, c).start()
    incoming[1, 0] = outgoing[1, spot]

    @pl.when(early)
    def _():
        for r in outside:
            slot_copy(0, r, 0).start()


    counts[0] = jnp.broadcast_to((own_tally + other_tally).astype(jnp.int32), (8, 128))
    count_copies = [
        remote(counts.at[0], counts.at[r], count_send.at[r], count_recv.at[r], address(ahead[r], member))
        for r in range(1, steps)
    ]
    for copy in count_copies:
        copy.start()

    out_bias = down_bias[pl.ds(place, 1), :]
    tile = min(TILE, hidden_units)

    def up(u, k, first):
        for t in range(groups):
            if first:
                with scope(f"upweight{t}"):
                    if t:
                        weight_copies[t - 1][0].wait_recv()
                        weight_copies[t - 1][1].wait_recv()
                    else:
                        own[0].wait()
            for i in range(hidden_units // tile):
                pre = jnp.dot(
                    incoming[u, pl.ds(k * near, near)].reshape(block, width),
                    up_all[t, :, i * tile : (i + 1) * tile],
                    preferred_element_type=jnp.float32,
                )
                pre = pre + bias_all[t, :, i * tile : (i + 1) * tile]
                begin = t * hidden_units + i * tile
                hidden[:, begin : begin + tile] = (
                    0.5 * pre * (1.0 + lax.erf(pre * 0.7071067811865476))
                ).astype(jnp.bfloat16)

    def back_copy(u, r, c):
        k = r // near
        columns = pl.ds(c * chunk, chunk)
        return remote(
            answers.at[u, r, :, columns],
            returned.at[u, k * near + spot, :, columns],
            back_send.at[u, r, c],
            back_recv.at[u, r, c],
            address(ahead[r], member),
        )

    def down(u, k, c):
        sums = out_bias[:, c * chunk : (c + 1) * chunk]
        for t in range(groups):
            sums = sums + jnp.dot(
                hidden[:, t * hidden_units : (t + 1) * hidden_units],
                down_all[t, :, c * chunk : (c + 1) * chunk],
                preferred_element_type=jnp.float32,
            )
        answers[u, pl.ds(k * near, near), :, c * chunk : (c + 1) * chunk] = sums.astype(
            jnp.bfloat16
        ).reshape(near, capacity, chunk)

    def arrived(u, c):
        for r in range(1, kept_steps):
            k, j = r // near, r % near
            columns = pl.ds(c * chunk, chunk)
            remote(
                answers.at[u, r, :, columns],
                returned.at[u, k * near + spots[j], :, columns],
                back_send.at[u, r, c],
                back_recv.at[u, r, c],
                address(ahead[r], member),
            ).wait_recv()

    def mixture(u, c):
        picked = returned[u, :, :, c * chunk : (c + 1) * chunk].reshape(slots, chunk)
        return jnp.dot(mix_high[u], picked, preferred_element_type=jnp.float32) + jnp.dot(
            mix_low[u], picked, preferred_element_type=jnp.float32
        )

    def rows_wait(u, k):
        for r in range(max(1, k * near), (k + 1) * near):
            for c in range(PIECES if u else 1):
                slot_copy(u, r, c).wait_recv()

    def back_start(u, k, c):
        for r in range(max(1, k * near), (k + 1) * near):
            back_copy(u, r, c).start()

    def by_member(ahead_item, behind_item, act, *more):
        if ahead_item == behind_item:
            act(*ahead_item, *more)
            return

        @pl.when(early)
        def _():
            act(*ahead_item, *more)

        @pl.when(late)
        def _():
            act(*behind_item, *more)

    far = range(1, bands)
    ahead_order = [(0, 0), (1, 0)] + [(1, k) for k in far] + [(0, k) for k in far]
    behind_order = [(0, 0)] + [(0, k) for k in far] + [(1, 0)] + [(1, k) for k in far]
    for step, (one, two) in enumerate(zip(ahead_order, behind_order)):
        u, k = (jnp.where(early, a, b) if a != b else a for a, b in zip(one, two))
        with scope(f"rows_{step}"):
            by_member(one, two, rows_wait)
        with scope(f"up_{step}"):
            up(u, k, step == 0)
        if step == 0:
            with scope("downweight"):
                own[1].wait()
                for copies in weight_copies:
                    copies[2].wait_recv()
        with scope(f"down_{step}"):
            for c in range(CHUNKS):
                down(u, k, c)
                by_member(one, two, back_start, c)
    for u in range(2):
        returned[u, spot] = answers[u, 0]

    def settle():
        for c in range(CHUNKS):
            with scope(f"arrived0{c}"):
                arrived(0, c)
            total[:, c * chunk : (c + 1) * chunk] = frames[
                :, c * chunk : (c + 1) * chunk
            ].astype(jnp.float32) + mixture(0, c)

    @pl.when(late)
    def _():
        settle()

    half_copies = [
        remote(halves.at[0, c], halves.at[1, c], half_send.at[c], half_recv.at[c], other)
        for c in range(CHUNKS)
    ]
    for c in range(CHUNKS):
        with scope(f"arrived1{c}"):
            arrived(1, c)
        halves[0, c] = mixture(1, c).astype(jnp.bfloat16)
        half_copies[c].start()

    with scope("counts"):
        for copy in count_copies:
            copy.wait()
    class_total = counts[0]
    for r in range(1, steps):
        class_total = class_total + counts[r]
    class_count[...] = class_total
    group_copies = [
        remote(class_count, group_counts.at[t], group_send.at[t], group_recv.at[t], address(place, peers[t]))
        for t in range(1, groups)
    ]
    for copy in group_copies:
        copy.start()

    @pl.when(early)
    def _():
        settle()

    with scope("groupwait"):
        for copy in group_copies:
            copy.wait()
    everything = class_count[...]
    for t in range(1, groups):
        everything = everything + group_counts[t]
    load[...] = everything

    fact_done = [copy for copies in weight_copies for copy in copies]
    for copy in fact_done:
        copy.wait_send()
    for r in inside:
        slot_copy(0, r, 0).wait_send()

    @pl.when(early)
    def _():
        for r in outside:
            slot_copy(0, r, 0).wait_send()

    for copy in shared_copies:
        copy.wait_send()

    for r in range(1, kept_steps):
        for c in range(PIECES):
            slot_copy(1, r, c).wait_send()
        for u in range(2):
            for c in range(CHUNKS):
                back_copy(u, r, c).wait_send()
    for c in range(CHUNKS):
        with scope(f"halfwait{c}"):
            half_copies[c].wait()
        mixed[:, c * chunk : (c + 1) * chunk] = (
            total[:, c * chunk : (c + 1) * chunk] + halves[1, c].astype(jnp.float32)
        ).astype(jnp.bfloat16)


def per_device(
    frames,
    norm_gain,
    norm_bias,
    routes,
    gate_codes,
    limits,
    up_weight,
    up_bias,
    down_weight,
    down_bias,
):
    owners = lax.axis_size("dp")
    holders = lax.axis_size("expert")
    expert_total = down_bias.shape[0]
    groups = owners * holders // expert_total
    frame_count, width = frames.shape
    capacity = 4 * frame_count // expert_total
    hidden_units = up_weight.shape[2]
    vmem = pl.BlockSpec(memory_space=pltpu.VMEM)
    anywhere = pl.BlockSpec(memory_space=pl.ANY)
    kept_steps = expert_total // 2
    slots = kept_steps * capacity
    blocks = (2, kept_steps, capacity, width)
    dma = pltpu.SemaphoreType.DMA
    mixed, load = pl.pallas_call(
        functools.partial(moe_kernel, owners, holders, groups, capacity),
        out_shape=(
            jax.ShapeDtypeStruct((frame_count, width), jnp.bfloat16),
            jax.ShapeDtypeStruct((8, 128), jnp.int32),
        ),
        in_specs=[
            pl.BlockSpec(memory_space=pltpu.SMEM),
            vmem,
            vmem,
            vmem,
            vmem,
            vmem,
            anywhere,
            vmem,
            anywhere,
            vmem,
        ],
        out_specs=(vmem, vmem),
        scratch_shapes=[
            pltpu.VMEM((groups, width, hidden_units), jnp.bfloat16),
            pltpu.VMEM((groups, hidden_units, width), jnp.bfloat16),
            pltpu.VMEM((groups, 1, hidden_units), jnp.float32),
            pltpu.VMEM((2, 8, frame_count), jnp.int32),
            pltpu.VMEM((2, PIECES, frame_count, width // PIECES), jnp.bfloat16),
            pltpu.VMEM(blocks, jnp.bfloat16),
            pltpu.VMEM(blocks, jnp.bfloat16),
            pltpu.VMEM((slots // (owners // 2), groups * hidden_units), jnp.bfloat16),
            pltpu.VMEM(blocks, jnp.bfloat16),
            pltpu.VMEM(blocks, jnp.bfloat16),
            pltpu.VMEM((2, CHUNKS, frame_count, width // CHUNKS), jnp.bfloat16),
            pltpu.VMEM((expert_total, 8, 128), jnp.int32),
            pltpu.VMEM((8, 128), jnp.int32),
            pltpu.VMEM((groups, 8, 128), jnp.int32),
            pltpu.VMEM((2, frame_count, slots), jnp.bfloat16),
            pltpu.VMEM((2, frame_count, slots), jnp.bfloat16),
            pltpu.VMEM((frame_count, width), jnp.float32),
            dma((2,)),
            dma((groups, 3)),
            dma((groups, 3)),
            dma(()),
            dma(()),
            dma((PIECES,)),
            dma((PIECES,)),
            dma((2, kept_steps, PIECES)),
            dma((2, kept_steps, PIECES)),
            dma((2, kept_steps, CHUNKS)),
            dma((2, kept_steps, CHUNKS)),
            dma((CHUNKS,)),
            dma((CHUNKS,)),
            dma((expert_total,)),
            dma((expert_total,)),
            dma((groups,)),
            dma((groups,)),
        ],
        compiler_params=pltpu.CompilerParams(
            collective_id=0, has_side_effects=True, vmem_limit_bytes=56 * 1024 * 1024
        ),
        name="moe",
    )(
        limits,
        frames,
        norm_gain.reshape(1, width),
        norm_bias.reshape(1, width),
        routes.T,
        gate_codes.T,
        up_weight,
        up_bias,
        down_weight,
        down_bias,
    )
    return (mixed, load[0, :expert_total])


def solution(mesh):
    in_specs = (
        P(("dp", "expert"), None),
        P(),
        P(),
        P(("dp", "expert"), None),
        P(("dp", "expert"), None),
        P(),
        P(("dp", "expert"), None, None),
        P(("dp", "expert"), None),
        P(("dp", "expert"), None, None),
        P(),
    )
    out_specs = (P(("dp", "expert"), None), P())
    return jax.shard_map(
        per_device, mesh=mesh, in_specs=in_specs, out_specs=out_specs, check_vma=False
    )
```

time: 58.3 us -> 54.2 us (0.930)
  the two profiles are of different devices: /device:TPU:0 before, /device:TPU:1 now
where the time goes in v1:
time: 54.2 us; the launch traced here: 54 us
  Pallas kernels  50.4 us (93%)
  local copies, waits for them, and re-layouts  2.86 us (5%)
  between operations  0.64 us (1%)
    pallas_call x1, Pallas kernels, per_device(): pl.pallas_call(functools.partial(moe_kernel, owners, holders, groups, cap...  50.4 us
    unnamed x1, local copies, waits for them, and re-layouts  1.67 us
    squeeze x1, local copies, waits for them, and re-layouts, per_device(): return (mixed, load[0, :expert_total])  1.2 us

profile of v1, /device:TPU:1, one launch (start us, length us, event | category | flops | bytes accessed | tf_op | source)
XLA Modules:
  0.0 54.0 jit_solution(12300049048634868196)
XLA Ops:
  0.6 50.4 %moe.1 = (bf16[128,1024]{1,0:T(8,128)(2,1)}, s32[8,128]{1,0:T(8,128)}) custom-call(s32[16]{0:T(128)} %limits.1, bf16[128,1024]{1,0:T(8,128)(2,1)} %frames.1, f32[1,1024]{1,0:T(1,128)} %bitcast.6, f32[1,1024]{1,0:T(1,128)} %bitcast.7, s32[2,128]{1,0:T(2,128)} %bitcast.8, s32[2,128]{1,0:T(2,128)} %bitcast.9, bf16[1,1024,2048]{2,1,0:T(8,128)(2,1)} %up_weight.1, ...), custom_call_target="tpu_custom_call" | custom-call | tf_op jit(solution)/shard_map/moe/pallas_call | solution.py:495
  51.1 1.2 %slice_bitcast_fusion = s32[16]{0:T(128)} fusion(s32[8,128]{1,0:T(8,128)} %get-tuple-element.5), kind=kLoop, calls=%fused_computation | loop fusion | bytes 128 | tf_op jit(solution)/shard_map/squeeze | solution.py:566
  52.3 1.7 %copy.13 = bf16[128,1024]{1,0:T(8,128)(2,1)} copy(bf16[128,1024]{1,0:T(8,128)(2,1)} %get-tuple-element.8) | data formatting | bytes 524288

commit v2 on v1

--- a/solution.py
+++ b/solution.py
@@ -261,20 +261,6 @@
         fact_copy.wait()
     with scope("places1"):
         other_picks, other_tally = places(1)
-    for c in range(PIECES):
-        with scope(f"sharedwait{c}"):
-            shared_copies[c].wait_recv()
-        fill(1, c * part, part, other_picks, shared[1, c])
-        for r in outside + inside:
-            slot_copy(1, r, c).start()
-    incoming[1, 0] = outgoing[1, spot]
-
-    @pl.when(early)
-    def _():
-        for r in outside:
-            slot_copy(0, r, 0).start()
-
-
     counts[0] = jnp.broadcast_to((own_tally + other_tally).astype(jnp.int32), (8, 128))
     count_copies = [
         remote(counts.at[0], counts.at[r], count_send.at[r], count_recv.at[r], address(ahead[r], member))
@@ -283,10 +269,17 @@
     for copy in count_copies:
         copy.start()
 
+    def pass_on(c):
+        with scope(f"sharedwait{c}"):
+            shared_copies[c].wait_recv()
+        fill(1, c * part, part, other_picks, shared[1, c])
+        for r in inside + outside:
+            slot_copy(1, r, c).start()
+
     out_bias = down_bias[pl.ds(place, 1), :]
     tile = min(TILE, hidden_units)
 
-    def up(u, k, first):
+    def up(u, k, at, first):
         for t in range(groups):
             if first:
                 with scope(f"upweight{t}"):
@@ -303,7 +296,7 @@
                 )
                 pre = pre + bias_all[t, :, i * tile : (i + 1) * tile]
                 begin = t * hidden_units + i * tile
-                hidden[:, begin : begin + tile] = (
+                hidden[at, :, begin : begin + tile] = (
                     0.5 * pre * (1.0 + lax.erf(pre * 0.7071067811865476))
                 ).astype(jnp.bfloat16)
 
@@ -318,11 +311,11 @@
             address(ahead[r], member),
         )
 
-    def down(u, k, c):
+    def down(u, k, at, c):
         sums = out_bias[:, c * chunk : (c + 1) * chunk]
         for t in range(groups):
             sums = sums + jnp.dot(
-                hidden[:, t * hidden_units : (t + 1) * hidden_units],
+                hidden[at, :, t * hidden_units : (t + 1) * hidden_units],
                 down_all[t, :, c * chunk : (c + 1) * chunk],
                 preferred_element_type=jnp.float32,
             )
@@ -357,51 +350,84 @@
         for r in range(max(1, k * near), (k + 1) * near):
             back_copy(u, r, c).start()
 
-    def by_member(ahead_item, behind_item, act, *more):
-        if ahead_item == behind_item:
-            act(*ahead_item, *more)
+    def by_member(one, two, act):
+        if one == two:
+            act(one)
             return
-
-        @pl.when(early)
-        def _():
-            act(*ahead_item, *more)
-
-        @pl.when(late)
-        def _():
-            act(*behind_item, *more)
-
-    far = range(1, bands)
-    ahead_order = [(0, 0), (1, 0)] + [(1, k) for k in far] + [(0, k) for k in far]
-    behind_order = [(0, 0)] + [(0, k) for k in far] + [(1, 0)] + [(1, k) for k in far]
-    for step, (one, two) in enumerate(zip(ahead_order, behind_order)):
-        u, k = (jnp.where(early, a, b) if a != b else a for a, b in zip(one, two))
-        with scope(f"rows_{step}"):
-            by_member(one, two, rows_wait)
-        with scope(f"up_{step}"):
-            up(u, k, step == 0)
-        if step == 0:
-            with scope("downweight"):
-                own[1].wait()
-                for copies in weight_copies:
-                    copies[2].wait_recv()
-        with scope(f"down_{step}"):
-            for c in range(CHUNKS):
-                down(u, k, c)
-                by_member(one, two, back_start, c)
-    for u in range(2):
-        returned[u, spot] = answers[u, 0]
-
-    def settle():
+        for item, mine in ((one, early), (two, late)):
+            if item is not None:
+                pl.when(mine)(functools.partial(act, item))
+
+    def both(one, two):
+        return [a if a == b else jnp.where(early, a, b) for a, b in zip(one, two)]
+
+    def rise(one, two):
+        def act(item):
+            with scope(f"up_{item[0]}{item[1]}"):
+                up(*item, False)
+
+        def rows(item):
+            with scope(f"rows_{item[0]}{item[1]}"):
+                rows_wait(item[0], item[1])
+
+        by_member(one, two, rows)
+        if one is None or two is None:
+            by_member(one, two, act)
+        else:
+            with scope("up"):
+                up(*both(one, two), one == two)
+
+    def fall(one, two):
         for c in range(CHUNKS):
-            with scope(f"arrived0{c}"):
-                arrived(0, c)
-            total[:, c * chunk : (c + 1) * chunk] = frames[
-                :, c * chunk : (c + 1) * chunk
-            ].astype(jnp.float32) + mixture(0, c)
+            if one is None or two is None:
+                by_member(one, two, lambda item: down(*item, c))
+            else:
+                with scope(f"down{c}"):
+                    down(*both(one, two), c)
+            by_member(one, two, lambda item: back_start(item[0], item[1], c))
+
+    def down_weights():
+        with scope("downweight"):
+            own[1].wait()
+            for copies in weight_copies:
+                copies[2].wait_recv()
+
+    def pass_all():
+        for c in range(PIECES):
+            pass_on(c)
+        incoming[1, 0] = outgoing[1, spot]
+
+    far = list(range(1, bands))
+    pl.when(early)(pass_all)
+    rise((0, 0, 0), (0, 0, 0))
+    rise((1, 0, 1), (0, 1, 1))
+    for k in far[1:]:
+        rise(None, (0, k, k))
+
+    @pl.when(early)
+    def _():
+        for r in outside:
+            slot_copy(0, r, 0).start()
 
     @pl.when(late)
     def _():
-        settle()
+        pass_all()
+        down_weights()
+
+    fall(None, (0, 0, 0))
+    rise((1, 1, bands), (1, 0, 0))
+    for k in far[1:]:
+        rise((1, k, bands - 1 + k), (1, k - 1, bands - 2 + k))
+    rise(None, (1, bands - 1, 2 * bands - 2))
+    pl.when(early)(down_weights)
+    for k in far:
+        fall((1, k, bands - 1 + k), (1, k, bands - 1 + k))
+    fall((1, 0, 1), (1, 0, 0))
+    returned[1, spot] = answers[1, 0]
+    fall((0, 0, 0), (0, 1, 1))
+    for k in far[1:]:
+        fall(None, (0, k, k))
+    returned[0, spot] = answers[0, 0]
 
     half_copies = [
         remote(halves.at[0, c], halves.at[1, c], half_send.at[c], half_recv.at[c], other)
@@ -412,6 +438,10 @@
             arrived(1, c)
         halves[0, c] = mixture(1, c).astype(jnp.bfloat16)
         half_copies[c].start()
+
+    for k in far:
+        rise((0, k, 0), None)
+        fall((0, k, 0), None)
 
     with scope("counts"):
         for copy in count_copies:
@@ -427,10 +457,12 @@
     for copy in group_copies:
         copy.start()
 
-    @pl.when(early)
-    def _():
-        settle()
-
+    for c in range(CHUNKS):
+        with scope(f"arrived0{c}"):
+            arrived(0, c)
+        total[:, c * chunk : (c + 1) * chunk] = frames[:, c * chunk : (c + 1) * chunk].astype(
+            jnp.float32
+        ) + mixture(0, c)
     with scope("groupwait"):
         for copy in group_copies:
             copy.wait()
@@ -465,6 +497,11 @@
         mixed[:, c * chunk : (c + 1) * chunk] = (
             total[:, c * chunk : (c + 1) * chunk] + halves[1, c].astype(jnp.float32)
         ).astype(jnp.bfloat16)
+
+
+def finish_kernel(mixed, load, mixed_out, load_out):
+    mixed_out[...] = mixed[...]
+    load_out[...] = load[0:1, 0 : load_out.shape[1]]
 
 
 def per_device(
@@ -495,8 +532,8 @@
     mixed, load = pl.pallas_call(
         functools.partial(moe_kernel, owners, holders, groups, capacity),
         out_shape=(
-            jax.ShapeDtypeStruct((frame_count, width), jnp.bfloat16),
-            jax.ShapeDtypeStruct((8, 128), jnp.int32),
+            pltpu.VMEM((frame_count, width), jnp.bfloat16),
+            pltpu.VMEM((8, 128), jnp.int32),
         ),
         in_specs=[
             pl.BlockSpec(memory_space=pltpu.SMEM),
@@ -519,7 +556,7 @@
             pltpu.VMEM((2, PIECES, frame_count, width // PIECES), jnp.bfloat16),
             pltpu.VMEM(blocks, jnp.bfloat16),
             pltpu.VMEM(blocks, jnp.bfloat16),
-            pltpu.VMEM((slots // (owners // 2), groups * hidden_units), jnp.bfloat16),
+            pltpu.VMEM((owners - 1, slots // (owners // 2), groups * hidden_units), jnp.bfloat16),
             pltpu.VMEM(blocks, jnp.bfloat16),
             pltpu.VMEM(blocks, jnp.bfloat16),
             pltpu.VMEM((2, CHUNKS, frame_count, width // CHUNKS), jnp.bfloat16),
@@ -563,7 +600,18 @@
         down_weight,
         down_bias,
     )
-    return (mixed, load[0, :expert_total])
+    mixed, load = pl.pallas_call(
+        finish_kernel,
+        out_shape=(
+            jax.ShapeDtypeStruct((frame_count, width), jnp.bfloat16),
+            jax.ShapeDtypeStruct((1, expert_total), jnp.int32),
+        ),
+        in_specs=[vmem, vmem],
+        out_specs=(vmem, vmem),
+        compiler_params=pltpu.CompilerParams(vmem_limit_bytes=2 * 1024 * 1024),
+        name="finish",
+    )(mixed, load)
+    return (mixed, load.reshape(expert_total))
 
 
 def solution(mesh):

time: 54.2 us -> 50.5 us (0.932)
  the two profiles are of different devices: /device:TPU:1 before, /device:TPU:0 now
where the time goes in v2:
time: 50.5 us; the launch traced here: 50.3 us
  Pallas kernels  49.7 us (98%)
  between operations  0.64 us (1%)
    pallas_call x1, Pallas kernels, per_device(): pl.pallas_call(functools.partial(moe_kernel, owners, holders, groups, cap...  49 us

profile of v2, /device:TPU:0, one launch (start us, length us, event | category | flops | bytes accessed | tf_op | source)
XLA Modules:
  0.0 50.3 jit_solution(5367678770829541389)
XLA Ops:
  0.6 49.0 %moe.1 = (bf16[128,1024]{1,0:T(8,128)(2,1)S(1)}, s32[8,128]{1,0:T(8,128)S(1)}) custom-call(s32[16]{0:T(128)} %limits.1, bf16[128,1024]{1,0:T(8,128)(2,1)} %frames.1, f32[1,1024]{1,0:T(1,128)} %bitcast.5, f32[1,1024]{1,0:T(1,128)} %bitcast.6, s32[2,128]{1,0:T(2,128)} %bitcast.7, s32[2,128]{1,0:T(2,128)} %bitcast.8, bf16[1,1024,2048]{2,1,0:T(8,128)(2,1)} %up_weight.1, ...), custom_call_target="tpu_custom_call" | custom-call | tf_op jit(solution)/shard_map/moe/pallas_call | solution.py:532
  49.6 0.7 %finish.1 = (bf16[128,1024]{1,0:T(8,128)(2,1)}, s32[1,16]{1,0:T(1,128)}) custom-call(bf16[128,1024]{1,0:T(8,128)(2,1)S(1)} %get-tuple-element.6.mixed, s32[8,128]{1,0:T(8,128)S(1)} %get-tuple-element.7.load), custom_call_target="tpu_custom_call" | custom-call | tf_op jit(solution)/shard_map/finish/pallas_call | solution.py:603

commit v3 on v2

--- a/solution.py
+++ b/solution.py
@@ -9,7 +9,8 @@
 epsilon = 1e-05
 TILE = 512
 PIECES = 4
-CHUNKS = 2
+CHUNKS = 4
+WIDE = 2
 
 
 def paired(value, step, size):
@@ -27,18 +28,25 @@
     holders,
     groups,
     capacity,
+    limits_in,
+    frames_in,
+    gain_in,
+    bias_in,
+    routes_in,
+    codes_in,
+    up_weight,
+    up_bias,
+    down_weight,
+    down_bias_in,
+    mixed,
+    load,
     limits,
     frames,
     gain,
     bias,
     routes,
     codes,
-    up_weight,
-    up_bias,
-    down_weight,
     down_bias,
-    mixed,
-    load,
     up_all,
     down_all,
     bias_all,
@@ -51,11 +59,13 @@
     returned,
     halves,
     counts,
+    half_counts,
     class_count,
     group_counts,
     mix_high,
     mix_low,
     total,
+    load_sem,
     own_sem,
     weight_send,
     weight_recv,
@@ -71,6 +81,8 @@
     half_recv,
     count_send,
     count_recv,
+    pair_send,
+    pair_recv,
     group_send,
     group_recv,
 ):
@@ -87,7 +99,6 @@
     frame_count, width = frames.shape
     hidden_units = up_weight.shape[2]
     bands = owners // 2
-    steps = owners * near
     kept_steps = bands * near
     slots = kept_steps * capacity
     block = near * capacity
@@ -115,7 +126,9 @@
     peers = [lax.rem(member + t, groups) for t in range(groups)]
 
     barrier = pltpu.get_barrier_semaphore()
-    for r in range(1, steps):
+    other = address(to_band[bands] * near + spot, member)
+    pl.semaphore_signal(barrier, inc=1, device_id=other, device_id_type=pl.DeviceIdType.MESH)
+    for r in range(1, kept_steps):
         pl.semaphore_signal(
             barrier, inc=1, device_id=address(ahead[r], member), device_id_type=pl.DeviceIdType.MESH
         )
@@ -123,16 +136,29 @@
         pl.semaphore_signal(
             barrier, inc=1, device_id=address(place, peers[t]), device_id_type=pl.DeviceIdType.MESH
         )
+    loads = [
+        pltpu.make_async_copy(source, target, load_sem.at[i])
+        for i, (source, target) in enumerate(
+            (
+                (frames_in, frames),
+                (gain_in, gain),
+                (bias_in, bias),
+                (routes_in, routes),
+                (codes_in, codes),
+                (limits_in, limits),
+                (up_bias, bias_all.at[0]),
+                (down_bias_in, down_bias),
+            )
+        )
+    ]
+    for copy in loads:
+        copy.start()
     own = [
         pltpu.make_async_copy(up_weight.at[0], up_all.at[0], own_sem.at[0]),
         pltpu.make_async_copy(down_weight.at[0], down_all.at[0], own_sem.at[1]),
     ]
-    for copy in own:
-        copy.start()
-    bias_all[0] = up_bias[...]
-    facts[0, 0:2, :] = routes[...]
-    facts[0, 2:4, :] = codes[...]
-    facts[0, 4:8, :] = jnp.zeros((4, frame_count), jnp.int32)
+    for copy in loads[:3]:
+        copy.wait()
 
     values = frames[...].astype(jnp.float32)
     center = jnp.mean(values, axis=-1, keepdims=True)
@@ -141,6 +167,13 @@
     normed = (shifted * lax.rsqrt(spread + epsilon) * gain[...] + bias[...]).astype(jnp.bfloat16)
     for c in range(PIECES):
         shared[0, c] = normed[:, c * part : (c + 1) * part]
+    for copy in loads[3:]:
+        copy.wait()
+    facts[0, 0:2, :] = routes[...]
+    facts[0, 2:4, :] = codes[...]
+    facts[0, 4:8, :] = jnp.zeros((4, frame_count), jnp.int32)
+    for copy in own:
+        copy.start()
 
     square = (frame_count, frame_count)
     across = lax.broadcasted_iota(jnp.int32, square, 1)
@@ -214,8 +247,7 @@
     outside = list(range(near, kept_steps))
 
     with scope("barrier"):
-        pl.semaphore_wait(barrier, steps - 1 + groups - 1)
-    other = address(to_band[bands] * near + spot, member)
+        pl.semaphore_wait(barrier, kept_steps + groups - 1)
     fact_copy = remote(facts.at[0], facts.at[1], fact_send, fact_recv, other)
     fact_copy.start()
     shared_copies = [
@@ -264,7 +296,7 @@
     counts[0] = jnp.broadcast_to((own_tally + other_tally).astype(jnp.int32), (8, 128))
     count_copies = [
         remote(counts.at[0], counts.at[r], count_send.at[r], count_recv.at[r], address(ahead[r], member))
-        for r in range(1, steps)
+        for r in range(1, kept_steps)
     ]
     for copy in count_copies:
         copy.start()
@@ -312,16 +344,17 @@
         )
 
     def down(u, k, at, c):
-        sums = out_bias[:, c * chunk : (c + 1) * chunk]
+        begin, end = c * width // WIDE, (c + 1) * width // WIDE
+        sums = out_bias[:, begin:end]
         for t in range(groups):
             sums = sums + jnp.dot(
                 hidden[at, :, t * hidden_units : (t + 1) * hidden_units],
-                down_all[t, :, c * chunk : (c + 1) * chunk],
+                down_all[t, :, begin:end],
                 preferred_element_type=jnp.float32,
             )
-        answers[u, pl.ds(k * near, near), :, c * chunk : (c + 1) * chunk] = sums.astype(
-            jnp.bfloat16
-        ).reshape(near, capacity, chunk)
+        answers[u, pl.ds(k * near, near), :, begin:end] = sums.astype(jnp.bfloat16).reshape(
+            near, capacity, end - begin
+        )
 
     def arrived(u, c):
         for r in range(1, kept_steps):
@@ -378,13 +411,14 @@
                 up(*both(one, two), one == two)
 
     def fall(one, two):
-        for c in range(CHUNKS):
+        for w in range(WIDE):
             if one is None or two is None:
-                by_member(one, two, lambda item: down(*item, c))
+                by_member(one, two, lambda item: down(*item, w))
             else:
-                with scope(f"down{c}"):
-                    down(*both(one, two), c)
-            by_member(one, two, lambda item: back_start(item[0], item[1], c))
+                with scope(f"down{w}"):
+                    down(*both(one, two), w)
+            for c in range(w * CHUNKS // WIDE, (w + 1) * CHUNKS // WIDE):
+                by_member(one, two, lambda item: back_start(item[0], item[1], c))
 
     def down_weights():
         with scope("downweight"):
@@ -400,34 +434,40 @@
     far = list(range(1, bands))
     pl.when(early)(pass_all)
     rise((0, 0, 0), (0, 0, 0))
-    rise((1, 0, 1), (0, 1, 1))
-    for k in far[1:]:
-        rise(None, (0, k, k))
 
     @pl.when(early)
     def _():
         for r in outside:
             slot_copy(0, r, 0).start()
 
-    @pl.when(late)
-    def _():
-        pass_all()
-        down_weights()
-
-    fall(None, (0, 0, 0))
+    rise((1, 0, 1), (0, 1, 1))
+    for k in far[1:]:
+        rise(None, (0, k, k))
+    pl.when(late)(pass_all)
+    down_weights()
+    fall((0, 0, 0), (0, 0, 0))
+    for k in far:
+        fall(None, (0, k, k))
+    for copy in count_copies:
+        copy.wait()
+    half_total = counts[0]
+    for r in range(1, kept_steps):
+        half_total = half_total + counts[r]
+    half_counts[0] = half_total
+    pair_copy = remote(half_counts.at[0], half_counts.at[1], pair_send, pair_recv, other)
+    pair_copy.start()
     rise((1, 1, bands), (1, 0, 0))
     for k in far[1:]:
         rise((1, k, bands - 1 + k), (1, k - 1, bands - 2 + k))
     rise(None, (1, bands - 1, 2 * bands - 2))
-    pl.when(early)(down_weights)
     for k in far:
         fall((1, k, bands - 1 + k), (1, k, bands - 1 + k))
     fall((1, 0, 1), (1, 0, 0))
-    returned[1, spot] = answers[1, 0]
-    fall((0, 0, 0), (0, 1, 1))
-    for k in far[1:]:
-        fall(None, (0, k, k))
-    returned[0, spot] = answers[0, 0]
+    for k in far:
+        rise((0, k, 0), None)
+        fall((0, k, 0), None)
+    for u in range(2):
+        returned[u, spot] = answers[u, 0]
 
     half_copies = [
         remote(halves.at[0, c], halves.at[1, c], half_send.at[c], half_recv.at[c], other)
@@ -439,17 +479,9 @@
         halves[0, c] = mixture(1, c).astype(jnp.bfloat16)
         half_copies[c].start()
 
-    for k in far:
-        rise((0, k, 0), None)
-        fall((0, k, 0), None)
-
     with scope("counts"):
-        for copy in count_copies:
-            copy.wait()
-    class_total = counts[0]
-    for r in range(1, steps):
-        class_total = class_total + counts[r]
-    class_count[...] = class_total
+        pair_copy.wait()
+    class_count[...] = half_counts[0] + half_counts[1]
     group_copies = [
         remote(class_count, group_counts.at[t], group_send.at[t], group_recv.at[t], address(place, peers[t]))
         for t in range(1, groups)
@@ -536,19 +568,26 @@
             pltpu.VMEM((8, 128), jnp.int32),
         ),
         in_specs=[
-            pl.BlockSpec(memory_space=pltpu.SMEM),
-            vmem,
-            vmem,
-            vmem,
-            vmem,
-            vmem,
-            anywhere,
-            vmem,
-            anywhere,
-            vmem,
+            anywhere,
+            anywhere,
+            anywhere,
+            anywhere,
+            anywhere,
+            anywhere,
+            anywhere,
+            anywhere,
+            anywhere,
+            anywhere,
         ],
         out_specs=(vmem, vmem),
         scratch_shapes=[
+            pltpu.SMEM((expert_total,), jnp.int32),
+            pltpu.VMEM((frame_count, width), jnp.bfloat16),
+            pltpu.VMEM((1, width), jnp.float32),
+            pltpu.VMEM((1, width), jnp.float32),
+            pltpu.VMEM((2, frame_count), jnp.int32),
+            pltpu.VMEM((2, frame_count), jnp.int32),
+            pltpu.VMEM((expert_total, width), jnp.float32),
             pltpu.VMEM((groups, width, hidden_units), jnp.bfloat16),
             pltpu.VMEM((groups, hidden_units, width), jnp.bfloat16),
             pltpu.VMEM((groups, 1, hidden_units), jnp.float32),
@@ -560,12 +599,14 @@
             pltpu.VMEM(blocks, jnp.bfloat16),
             pltpu.VMEM(blocks, jnp.bfloat16),
             pltpu.VMEM((2, CHUNKS, frame_count, width // CHUNKS), jnp.bfloat16),
-            pltpu.VMEM((expert_total, 8, 128), jnp.int32),
+            pltpu.VMEM((kept_steps, 8, 128), jnp.int32),
+            pltpu.VMEM((2, 8, 128), jnp.int32),
             pltpu.VMEM((8, 128), jnp.int32),
             pltpu.VMEM((groups, 8, 128), jnp.int32),
             pltpu.VMEM((2, frame_count, slots), jnp.bfloat16),
             pltpu.VMEM((2, frame_count, slots), jnp.bfloat16),
             pltpu.VMEM((frame_count, width), jnp.float32),
+            dma((8,)),
             dma((2,)),
             dma((groups, 3)),
             dma((groups, 3)),
@@ -579,8 +620,10 @@
             dma((2, kept_steps, CHUNKS)),
             dma((CHUNKS,)),
             dma((CHUNKS,)),
-            dma((expert_total,)),
-            dma((expert_total,)),
+            dma((kept_steps,)),
+            dma((kept_steps,)),
+            dma(()),
+            dma(()),
             dma((groups,)),
             dma((groups,)),
         ],

time: 50.5 us -> 47.2 us (0.935); the launches traced: 50.3 us -> 46.5 us
  Pallas kernels: 49.7 us -> 45.8 us
    pallas_call x1, Pallas kernels: 49 us -> 45.1 us  [per_device(): pl.pallas_call(functools.partial(moe_kernel, owners, holders, groups, cap...]
where the time goes in v3:
time: 47.2 us; the launch traced here: 46.5 us
  Pallas kernels  45.8 us (97%)
  between operations  0.64 us (1%)
    pallas_call x1, Pallas kernels, per_device(): pl.pallas_call(functools.partial(moe_kernel, owners, holders, groups, cap...  45.1 us

profile of v3, /device:TPU:0, one launch (start us, length us, event | category | flops | bytes accessed | tf_op | source)
XLA Modules:
  0.0 46.5 jit_solution(10774135821256655633)
XLA Ops:
  0.6 45.1 %moe.1 = (bf16[128,1024]{1,0:T(8,128)(2,1)S(1)}, s32[8,128]{1,0:T(8,128)S(1)}) custom-call(s32[16]{0:T(128)} %limits_in.1, bf16[128,1024]{1,0:T(8,128)(2,1)} %frames_in.1, f32[1,1024]{1,0:T(1,128)} %bitcast.5, f32[1,1024]{1,0:T(1,128)} %bitcast.6, s32[2,128]{1,0:T(2,128)} %bitcast.7, s32[2,128]{1,0:T(2,128)} %bitcast.8, bf16[1,1024,2048]{2,1,0:T(8,128)(2,1)} %up_weight.1, ...), custom_call_target="tpu_custom_call" | custom-call | tf_op jit(solution)/shard_map/moe/pallas_call | solution.py:564
  45.7 0.7 %finish.1 = (bf16[128,1024]{1,0:T(8,128)(2,1)}, s32[1,16]{1,0:T(1,128)}) custom-call(bf16[128,1024]{1,0:T(8,128)(2,1)S(1)} %get-tuple-element.6.mixed, s32[8,128]{1,0:T(8,128)S(1)} %get-tuple-element.7.load), custom_call_target="tpu_custom_call" | custom-call | tf_op jit(solution)/shard_map/finish/pallas_call | solution.py:646

commit v4 on v3

--- a/solution.py
+++ b/solution.py
@@ -305,7 +305,7 @@
         with scope(f"sharedwait{c}"):
             shared_copies[c].wait_recv()
         fill(1, c * part, part, other_picks, shared[1, c])
-        for r in inside + outside:
+        for r in outside + inside:
             slot_copy(1, r, c).start()
 
     out_bias = down_bias[pl.ds(place, 1), :]

time: 47.2 us -> 47.2 us (level)
  no operation moved by 1% of the time
where the time goes in v4:
time: 47.2 us; the launch traced here: 46.4 us
  Pallas kernels  45.8 us (97%)
  between operations  0.64 us (1%)
    pallas_call x1, Pallas kernels, per_device(): pl.pallas_call(functools.partial(moe_kernel, owners, holders, groups, cap...  45.1 us

profile of v4, /device:TPU:0, one launch (start us, length us, event | category | flops | bytes accessed | tf_op | source)
XLA Modules:
  0.0 46.4 jit_solution(4386417214223396368)
XLA Ops:
  0.6 45.1 %moe.1 = (bf16[128,1024]{1,0:T(8,128)(2,1)S(1)}, s32[8,128]{1,0:T(8,128)S(1)}) custom-call(s32[16]{0:T(128)} %limits_in.1, bf16[128,1024]{1,0:T(8,128)(2,1)} %frames_in.1, f32[1,1024]{1,0:T(1,128)} %bitcast.5, f32[1,1024]{1,0:T(1,128)} %bitcast.6, s32[2,128]{1,0:T(2,128)} %bitcast.7, s32[2,128]{1,0:T(2,128)} %bitcast.8, bf16[1,1024,2048]{2,1,0:T(8,128)(2,1)} %up_weight.1, ...), custom_call_target="tpu_custom_call" | custom-call | tf_op jit(solution)/shard_map/moe/pallas_call | solution.py:564
  45.7 0.7 %finish.1 = (bf16[128,1024]{1,0:T(8,128)(2,1)}, s32[1,16]{1,0:T(1,128)}) custom-call(bf16[128,1024]{1,0:T(8,128)(2,1)S(1)} %get-tuple-element.6.mixed, s32[8,128]{1,0:T(8,128)S(1)} %get-tuple-element.7.load), custom_call_target="tpu_custom_call" | custom-call | tf_op jit(solution)/shard_map/finish/pallas_call | solution.py:646
